TPU v7x, 32 devices: a whole 2x2x4 slice. The times are simulated.
32 devices in a mesh: dp: 4 (over y, x), owner: 8 (over z, core).
Axes of the slice: x: 2, y: 2, z: 4, core: 2. Of those that a mesh axis runs over, the one named last changes fastest.
Arguments:
- partial_grads: bfloat16 [4, 48, 1024, 1024], P('dp', None, 'owner'), may hold values from -2.09375 to 2.09375
- owner_map: int32 [48], replicated, may hold values from 0 to 7, as said below
- left_stats: float32 [8, 12, 1024, 1024], P('owner', None, 'dp'), may hold values from -1.8 to 1.8
- right_stats: float32 [8, 12, 1024, 1024], P('owner', None, 'dp'), may hold values from -1.8 to 1.8
- left_roots: bfloat16 [8, 12, 1024, 1024], P('owner', None, 'dp'), as said below
- right_roots: bfloat16 [8, 12, 1024, 1024], P('owner', None, 'dp'), as said below
Outputs:
- direction: bfloat16 [48, 1024, 1024], P(None, ('dp', 'owner'))
- new_left_stats: float32 [8, 12, 1024, 1024], P('owner', None, 'dp')
- new_right_stats: float32 [8, 12, 1024, 1024], P('owner', None, 'dp')
Inputs may be any that keep to these rules, and one draw needn't show every extreme that they name: `owner_map`: no owner index holds more than 12 blocks, and some owner holds exactly 12. `left_roots`: each block is dense and not symmetric; its diagonal entries are of order one and its off-diagonal entries are small. `right_roots`: each block is dense and not symmetric; its diagonal entries are of order one and its off-diagonal entries are small.
All inputs are finite; a program needn't handle non-finite values.
Results may differ from a plain program's by a relative error of at most 0.017.
Values may be sent and summed in bfloat16 or wider, within the bound.
A program may use at most 256 MiB of HBM per device.

v0:
```python
import jax
import jax.numpy as jnp
from jax import lax
from jax.sharding import PartitionSpec as P

D_MODEL = 2560
D_IN = 10576
D_INNER = 5120
TILE = 1024


stat_decay = 0.999


def extents(count):
    index = jnp.arange(count, dtype=jnp.int32)
    in_cols = -(-D_IN // TILE)
    out_cols = -(-D_MODEL // TILE)
    in_count = -(-D_MODEL // TILE) * in_cols
    is_in = index < in_count
    other = jnp.maximum(index - in_count, 0)
    rows = jnp.where(
        is_in,
        jnp.minimum(TILE, D_MODEL - index // in_cols * TILE),
        jnp.minimum(TILE, D_INNER - other // out_cols * TILE),
    )
    cols = jnp.where(
        is_in,
        jnp.minimum(TILE, D_IN - index % in_cols * TILE),
        jnp.minimum(TILE, D_MODEL - other % out_cols * TILE),
    )
    return (rows, cols)


def body(partial_grads, owner_map, left_stats, right_stats, left_roots, right_roots):
    owners = lax.axis_size("owner")
    owner_here = lax.axis_index("owner")
    dp_here = lax.axis_index("dp")
    tiles = owner_map.shape[0]
    slots = left_stats.shape[1]
    lanes = left_stats.shape[2]
    tile = left_stats.shape[3]
    piece = partial_grads.shape[2]
    rows, cols = extents(tiles)
    line = jnp.arange(tile, dtype=jnp.int32)
    piece_rows = owner_here * piece + jnp.arange(piece, dtype=jnp.int32)
    source_mask = (piece_rows[None, :, None] < rows[:, None, None]) & (
        line[None, None, :] < cols[:, None, None]
    )
    local = jnp.where(source_mask, partial_grads[0], jnp.zeros((), jnp.bfloat16))
    ids = jnp.arange(tiles, dtype=jnp.int32)
    same = (owner_map[:, None] == owner_map[None, :]) & (ids[None, :] < ids[:, None])
    slot = jnp.sum(same.astype(jnp.int32), axis=1)
    picks = (slot[None, None, :] == jnp.arange(slots, dtype=jnp.int32)[:, None, None]) & (
        owner_map[None, None, :] == jnp.arange(owners, dtype=jnp.int32)[None, :, None]
    )
    tile_of = jnp.sum(jnp.where(picks, ids[None, None, :], 0), axis=2)
    filled = jnp.any(picks, axis=2)
    shares = lax.psum_scatter(
        local.astype(jnp.float32).astype(jnp.bfloat16), "dp", scatter_dimension=1, tiled=True
    )
    taken = jnp.take(shares, tile_of.reshape(-1), axis=0)
    taken = taken.reshape((slots, owners) + shares.shape[1:])
    arrived = lax.all_to_all(
        jnp.where(filled[:, :, None, None], taken, jnp.zeros((), shares.dtype)),
        "owner",
        split_axis=1,
        concat_axis=1,
        tiled=True,
    )
    grads = lax.all_gather(arrived, "dp", axis=2, tiled=True).reshape(slots, tile, tile)
    grad_rows = lax.dynamic_slice_in_dim(grads, dp_here * lanes, lanes, 1)
    grad_cols = lax.dynamic_slice_in_dim(grads, dp_here * lanes, lanes, 2)
    left_gram = jnp.einsum("srk,stk->srt", grad_rows, grads, preferred_element_type=jnp.float32)
    right_gram = jnp.einsum("skc,skt->sct", grad_cols, grads, preferred_element_type=jnp.float32)
    new_left = stat_decay * left_stats[0] + (1.0 - stat_decay) * left_gram
    new_right = stat_decay * right_stats[0] + (1.0 - stat_decay) * right_gram
    left_part = jnp.einsum(
        "srk,skc->src", left_roots[0], grads, preferred_element_type=jnp.float32
    ).astype(jnp.bfloat16)
    product = jnp.einsum(
        "srk,skc->src",
        left_part,
        lax.all_gather(right_roots[0], "dp", axis=1, tiled=True),
        preferred_element_type=jnp.float32,
    )
    tile_here = lax.dynamic_index_in_dim(tile_of, owner_here, 1, keepdims=False)
    rows_here = jnp.take(rows, tile_here)
    cols_here = jnp.take(cols, tile_here)
    block_rows = dp_here * lanes + jnp.arange(lanes, dtype=jnp.int32)
    out_mask = (block_rows[None, :, None] < rows_here[:, None, None]) & (
        line[None, None, :] < cols_here[:, None, None]
    )
    result = jnp.where(out_mask, product, jnp.float32(0.0)).astype(jnp.bfloat16)
    sub_rows = lanes // owners
    returned = lax.all_to_all(
        result.reshape(slots, owners, sub_rows, tile),
        "owner",
        split_axis=1,
        concat_axis=1,
        tiled=True,
    )
    flat = returned.reshape(slots * owners, sub_rows, tile)
    direction = jnp.take(flat, slot * owners + owner_map, axis=0)
    return (direction, new_left[None], new_right[None])


def solution(mesh):
    placed = (
        P("dp", None, "owner", None),
        P(),
        P("owner", None, "dp", None),
        P("owner", None, "dp", None),
        P("owner", None, "dp", None),
        P("owner", None, "dp", None),
    )
    return jax.shard_map(
        body,
        mesh=mesh,
        in_specs=placed,
        out_specs=(
            P(None, ("dp", "owner"), None),
            P("owner", None, "dp", None),
            P("owner", None, "dp", None),
        ),
        check_vma=False,
    )
```

profile of v0, /device:TPU:0, one launch (start us, length us, event | category | flops | bytes accessed | tf_op | source)
XLA Modules:
  0.0 949.2 jit_solution(2275614357485524921)
XLA Ops:
  7.2 0.0 reduce-scatter.2.cloned.1.call-start
  7.2 0.1 iota_compare_fusion
  7.4 0.1 broadcast_compare_fusion
  7.4 12.1 %and_select_fusion = bf16[48,128,1024]{2,1,0:T(8,128)(2,1)} fusion(bf16[1,48,128,1024]{3,2,1,0:T(8,128)(2,1)} %param.8, pred[48,1024]{1,0:T(8,128)(4,1)S(1)} %iota_compare_fusion, pred[48,128]{1,0:T(8,128)(4,1)S(1)} %broadcast_compare_fusion), kind=kLoop, calls=%fused_computation.6 | loop fusion | flops 12582912 | bytes 25221120 | tf_op jit(solution)/shard_map/jit(_where)/select_n | solution.py:50
  19.5 0.0 copy-start
  19.5 0.0 reduce-scatter.2.cloned.1.call-update
  19.5 0.0 all-gather.4.cloned.1.call-start
  19.6 0.6 copy-done
  20.2 0.2 convert_reduce_fusion
  20.4 0.3 fusion.25
  20.7 0.1 reshape.284
  20.8 0.3 and_reduce_fusion
  21.1 121.9 %reduce-scatter.2.cloned.1.call-done = bf16[48,32,1024]{2,1,0:T(8,128)(2,1)} async-done(((bf16[48,128,1024]{2,1,0:T(8,128)(2,1)}), bf16[48,32,1024]{2,1,0:T(8,128)(2,1)}) %reduce-scatter.2.cloned.1.call-update) | async-done | bytes 3145744 | tf_op jit(solution)/shard_map/reduce_scatter | solution.py:59
  143.0 7.9 gather_fusion
  150.9 4.0 select_select_fusion
  154.9 1.3 copy.27
  156.2 143.4 %all_to_all.10 = bf16[12,8,32,1024]{3,2,0,1:T(8,128)(2,1)} all-to-all(bf16[12,8,32,1024]{3,2,0,1:T(8,128)(2,1)S(1)} %copy.27), channel_id=1, replica_groups=mesh['dp'=4,'owner'=8] {'owner'}, dimensions={1} | all-to-all | bytes 12582912 | tf_op jit(solution)/shard_map/all_to_all | solution.py:64
  299.7 0.0 all-gather.4.cloned.1.call-update
  299.7 0.0 all-gather.6.cloned.1.call-start
  299.7 0.7 all-gather.6.cloned.1.call-update
  300.4 0.2 dynamic-slice_reduce_fusion
  300.6 0.7 gather_fusion.3
  301.3 0.7 gather_fusion.2
  302.0 0.1 broadcast_compare_fusion.1
  302.1 0.1 iota_compare_fusion.1
  302.2 223.2 %all-gather.4.cloned.1.call-done = bf16[12,8,128,1024]{3,2,0,1:T(8,128)(2,1)} async-done(((bf16[12,8,32,1024]{3,2,0,1:T(8,128)(2,1)}), bf16[12,8,128,1024]{3,2,0,1:T(8,128)(2,1)}) %all-gather.4.cloned.1.call-update) | async-done | bytes 25165840 | tf_op jit(solution)/shard_map/all_gather | solution.py:71
  525.4 34.1 %copy.28 = bf16[12,8,128,1024]{2,1,3,0:T(8,128)(2,1)} copy(bf16[12,8,128,1024]{3,2,0,1:T(8,128)(2,1)} %all-gather.4.cloned.1.call-done) | data formatting | bytes 50331648 | tf_op jit(solution)/shard_map/all_gather | solution.py:71
  559.5 37.4 %reshape.285 = bf16[12,1024,1024]{1,2,0:T(8,128)(2,1)} reshape(bf16[12,8,128,1024]{2,1,3,0:T(8,128)(2,1)} %copy.28) | data formatting | bytes 50331648 | tf_op jit(solution)/shard_map/reshape | solution.py:71
  596.9 158.0 %all-gather.6.cloned.1.call-done = bf16[1,12,1024,1024]{3,2,1,0:T(8,128)(2,1)} async-done(((bf16[1,12,256,1024]{3,2,1,0:T(8,128)(2,1)}), bf16[1,12,1024,1024]{3,2,1,0:T(8,128)(2,1)}) %all-gather.6.cloned.1.call-update) | async-done | bytes 25165840 | tf_op jit(solution)/shard_map/all_gather | solution.py:84
  754.9 25.0 %select_convert_fusion = bf16[12,256,1024]{2,1,0:T(8,128)(2,1)} fusion(pred[12,1024]{1,0:T(8,128)(4,1)S(1)} %iota_compare_fusion.1, pred[12,256]{1,0:T(8,128)(4,1)S(1)} %broadcast_compare_fusion.1, bf16[1,12,1024,1024]{3,2,1,0:T(8,128)(2,1)} %all-gather.6.cloned.1.call-done, bf16[12,1024,1024]{1,2,0:T(8,128)(2,1)} %reshape.285, ...), kind=kOutput, calls=%fused_computation.11 | convolution fusion | flops 12897484800 | bytes 62929920 | tf_op jit(solution)/shard_map/srk,skc->src/dot_general | solution.py:81
  779.9 6.8 copy.30
  786.6 4.9 all-to-all-start.1
  791.6 20.5 %fusion.3 = f32[1,12,256,1024]{3,2,1,0:T(8,128)} fusion(f32[1,12,256,1024]{3,2,1,0:T(8,128)} %param.10, bf16[12,1024,1024]{1,2,0:T(8,128)(2,1)} %reshape.285, s32[]{:T(128)S(6)} %select_n.138), kind=kOutput, calls=%fused_computation.10 | convolution fusion | flops 6451888128 | bytes 56623108 | tf_op jit(solution)/shard_map/srk,stk->srt/dot_general | solution.py:74
  812.1 20.2 %fusion.2 = f32[1,12,256,1024]{3,2,1,0:T(8,128)} fusion(f32[1,12,256,1024]{3,2,1,0:T(8,128)} %param.11, bf16[12,1024,1024]{1,2,0:T(8,128)(2,1)} %reshape.285, s32[]{:T(128)S(6)} %select_n.138), kind=kOutput, calls=%fused_computation.8 | convolution fusion | flops 6451888128 | bytes 56623108 | tf_op jit(solution)/shard_map/skc,skt->sct/dot_general | solution.py:75
  832.2 98.1 %all-to-all-done.1 = bf16[12,8,32,1024]{3,2,0,1:T(8,128)(2,1)} async-done(((bf16[12,8,32,1024]{3,2,0,1:T(8,128)(2,1)}), bf16[12,8,32,1024]{3,2,0,1:T(8,128)(2,1)}, u32[]{:S(2)}, u32[]{:S(2)}) %all-to-all-start.1) | async-done | bytes 6291488 | tf_op jit(solution)/shard_map/all_to_all | solution.py:96
  930.3 6.8 copy.31
  937.1 3.5 gather_fusion.1
  940.6 2.0 broadcast_select_fusion
  (13 shorter events, 0.1 us)
Async XLA Ops:
  7.2 135.8 %reduce-scatter.2.cloned.1.call-start = ((), (), s32[]{:S(2)}) async-start(), calls=%async_computation.3 | async-start | bytes 15728640 | tf_op jit(solution)/shard_map/reduce_scatter | solution.py:59
  19.5 0.7 copy-start
  19.5 505.8 %all-gather.4.cloned.1.call-start = ((), (), s32[]{:S(2)}) async-start(), calls=%async_computation.4 | async-start | bytes 31457280 | tf_op jit(solution)/shard_map/all_gather | solution.py:71
  299.7 455.2 %all-gather.6.cloned.1.call-start = ((), (), s32[]{:S(2)}) async-start(), calls=%async_computation.5 | async-start | bytes 31457280 | tf_op jit(solution)/shard_map/all_gather | solution.py:84
  786.6 143.7 %all-to-all-start.1 = ((bf16[12,8,32,1024]{3,2,0,1:T(8,128)(2,1)}), bf16[12,8,32,1024]{3,2,0,1:T(8,128)(2,1)}, u32[]{:S(2)}, u32[]{:S(2)}) async-start(bf16[12,8,32,1024]{3,2,0,1:T(8,128)(2,1)} %copy.30), calls=%async_computation.2 | async-start | bytes 12582912 | tf_op jit(solution)/shard_map/all_to_all | solution.py:96
Sparse Core Ops, SparseCore 0:
  19.7 123.2 reduce-scatter.1
  299.8 225.5 all-gather.3
  527.3 227.5 all-gather.5
where the time goes:
time: 951 us; the launch traced here: 949 us
  waiting for transfers between devices  602 us (63%)
  blocking collectives  143 us (15%)
  local copies, waits for them, and re-layouts  100 us (11%)
  matrix products  65.6 us (7%)
  other arithmetic  19.2 us (2%)
  between operations  13.9 us (1%)
    all_gather x1, waiting for transfers between devices, body(): lax.all_gather(arrived, 'dp', axis=2, tiled=True).reshape(slots, tile, tile)  223 us
    all_gather x1, waiting for transfers between devices, body(): lax.all_gather(right_roots[0], 'dp', axis=1, tiled=True)  158 us
    all_to_all x1, blocking collectives, body(): lax.all_to_all(jnp.where(filled[:, :, None, None], taken, jnp.zeros((), s...  143 us
    reduce_scatter x1, waiting for transfers between devices, body(): lax.psum_scatter(local.astype(jnp.float32).astype(jnp.bfloat16), 'dp', sc...  122 us
    all_to_all x1, waiting for transfers between devices, body(): lax.all_to_all(result.reshape(slots, owners, sub_rows, tile), 'owner', sp...  98.1 us
    reshape x1, local copies, waits for them, and re-layouts, body(): lax.all_gather(arrived, 'dp', axis=2, tiled=True).reshape(slots, tile, tile)  37.4 us
    all_gather x1, local copies, waits for them, and re-layouts, body(): lax.all_gather(arrived, 'dp', axis=2, tiled=True).reshape(slots, tile, tile)  34.1 us
    dot_general x1, matrix products, body(): jnp.einsum('srk,skc->src', left_part, lax.all_gather(right_roots[0], 'dp'...  25 us
  transfers between devices with their start and end apart: 4, of which 4 were waited for; matrix products, arithmetic and copies ran while one was open for 12% of the time, Pallas kernels for 0%

commit v1 on v0

v1 whole, which is shorter than its diff:
```python
import functools

import jax
import jax.numpy as jnp
from jax import lax
from jax.experimental import pallas as pl
from jax.experimental.pallas import tpu as pltpu
from jax.sharding import PartitionSpec as P


D_MODEL = 2560
D_IN = 10576
D_INNER = 5120
TILE = 1024

CHUNK = 3

stat_decay = 0.999


def extents(count):
    index = jnp.arange(count, dtype=jnp.int32)
    in_cols = -(-D_IN // TILE)
    out_cols = -(-D_MODEL // TILE)
    in_count = -(-D_MODEL // TILE) * in_cols
    is_in = index < in_count
    other = jnp.maximum(index - in_count, 0)
    rows = jnp.where(
        is_in,
        jnp.minimum(TILE, D_MODEL - index // in_cols * TILE),
        jnp.minimum(TILE, D_INNER - other // out_cols * TILE),
    )
    cols = jnp.where(
        is_in,
        jnp.minimum(TILE, D_IN - index % in_cols * TILE),
        jnp.minimum(TILE, D_MODEL - other % out_cols * TILE),
    )
    return (rows, cols)


def dot(a, b, dims):
    return lax.dot_general(a, b, (dims, ((), ())), preferred_element_type=jnp.float32)


def step_kernel(base, info, grads, roots, left_roots, left_stats, right_stats, *rest):
    direction, new_left, new_right, left_part = rest[-4:]
    dp, _, _, piece, width = grads.shape
    lanes, tile = left_stats.shape[1:]
    here = info[0]
    pieces = lanes // piece
    full = [grads[d].reshape(tile, width) for d in range(dp)]
    mine = grads[here].reshape(tile, width).T
    gram = None
    for d in range(dp):
        right = dot(mine, full[d], ((1,), (0,)))
        cut = (0, slice(None), slice(d * width, (d + 1) * width))
        new_right[cut] = stat_decay * right_stats[cut] + (1.0 - stat_decay) * right
        part = dot(left_roots[0], full[d], ((1,), (0,)))
        left_part[:, d * width : (d + 1) * width] = part.astype(jnp.bfloat16)
        rows = grads[d, pl.ds(here * pieces, pieces)].reshape(lanes, width)
        term = dot(rows, full[d], ((1,), (1,)))
        gram = term if gram is None else gram + term
    new_left[0] = stat_decay * left_stats[0] + (1.0 - stat_decay) * gram
    product = dot(left_part[...], roots[...].reshape(tile, tile), ((1,), (0,)))
    slot = base + pl.program_id(0)
    row = lax.broadcasted_iota(jnp.int32, product.shape, 0)
    col = lax.broadcasted_iota(jnp.int32, product.shape, 1)
    keep = (row < info[1 + 2 * slot]) & (col < info[2 + 2 * slot])
    result = jnp.where(keep, product, 0.0).astype(jnp.bfloat16)
    direction[...] = result.reshape(direction.shape)


def step(base, chunk, info, grads, roots, left_roots, left_stats, right_stats, carried):
    dp, owners, _, piece, width = grads.shape
    _, lanes, tile = left_stats.shape
    at = lambda s, info: (base + s, 0, 0)
    stats = pl.BlockSpec((1, lanes, tile), at)
    in_specs = [
        pl.BlockSpec((dp, owners, 1, piece, width), lambda s, info: (0, 0, s, 0, 0)),
        pl.BlockSpec((dp, 1, lanes, tile), lambda s, info: (0, base + s, 0, 0)),
        stats,
        stats,
        stats,
    ] + [pl.BlockSpec(memory_space=pl.ANY)] * len(carried)
    sub = lanes // owners
    return pl.pallas_call(
        functools.partial(step_kernel, base),
        grid_spec=pltpu.PrefetchScalarGridSpec(
            num_scalar_prefetch=1,
            grid=(chunk,),
            in_specs=in_specs,
            out_specs=[
                pl.BlockSpec((owners, 1, sub, tile), lambda s, info: (0, s, 0, 0)),
                stats,
                stats,
            ],
            scratch_shapes=[pltpu.VMEM((lanes, tile), jnp.bfloat16)],
        ),
        out_shape=[
            jax.ShapeDtypeStruct((owners, chunk, sub, tile), jnp.bfloat16),
            jax.ShapeDtypeStruct(left_stats.shape, jnp.float32),
            jax.ShapeDtypeStruct(right_stats.shape, jnp.float32),
        ],
        input_output_aliases={6: 1, 7: 2} if carried else {},
        compiler_params=pltpu.CompilerParams(vmem_limit_bytes=48 * 1024 * 1024),
        cost_estimate=pl.CostEstimate(
            flops=8 * chunk * lanes * tile * tile,
            bytes_accessed=chunk * (4 * tile * tile + 20 * lanes * tile),
            transcendentals=0,
        ),
    )(info, grads, roots, left_roots, left_stats, right_stats, *carried)


def inner(partial_grads, owner_map, left_stats, right_stats, left_roots, right_roots):
    dp = lax.axis_size("dp")
    owners = lax.axis_size("owner")
    owner_here = lax.axis_index("owner")
    dp_here = lax.axis_index("dp")
    tiles = owner_map.shape[0]
    slots = left_stats.shape[1]
    lanes = left_stats.shape[2]
    tile = left_stats.shape[3]
    piece = partial_grads.shape[2]
    width = tile // dp
    rows, cols = extents(tiles)
    ids = jnp.arange(tiles, dtype=jnp.int32)
    same = (owner_map[:, None] == owner_map[None, :]) & (ids[None, :] < ids[:, None])
    slot = jnp.sum(same.astype(jnp.int32), axis=1)
    picks = (slot[None, None, :] == jnp.arange(slots, dtype=jnp.int32)[None, :, None]) & (
        owner_map[None, None, :] == jnp.arange(owners, dtype=jnp.int32)[:, None, None]
    )
    tile_of = jnp.sum(jnp.where(picks, ids[None, None, :], 0), axis=2)
    filled = jnp.any(picks, axis=2)

    shares = lax.psum_scatter(partial_grads[0], "dp", scatter_dimension=2, tiled=True)
    roots = lax.all_gather(right_roots[0], "dp", axis=0)

    piece_rows = owner_here * piece + jnp.arange(piece, dtype=jnp.int32)
    piece_cols = dp_here * width + jnp.arange(width, dtype=jnp.int32)
    tile_here = lax.dynamic_index_in_dim(tile_of, owner_here, 0, keepdims=False)
    info = jnp.stack([jnp.take(rows, tile_here) - dp_here * lanes, jnp.take(cols, tile_here)], 1)
    info = jnp.concatenate([dp_here[None], info.reshape(-1)]).astype(jnp.int32)

    chunk = CHUNK if slots % CHUNK == 0 else 1
    arrived = []
    for base in range(0, slots, chunk):
        which = tile_of[:, base : base + chunk]
        rows_of = jnp.where(filled[:, base : base + chunk], jnp.take(rows, which), 0)
        mask = (piece_rows[:, None] < rows_of[:, :, None, None]) & (
            piece_cols[None, :] < jnp.take(cols, which)[:, :, None, None]
        )
        taken = jnp.take(shares, which.reshape(-1), axis=0).reshape(owners, chunk, piece, width)
        sent = lax.all_to_all(
            jnp.where(mask, taken, jnp.zeros((), shares.dtype)),
            "owner",
            split_axis=0,
            concat_axis=0,
            tiled=True,
        )
        arrived.append(sent)

    def place(index, returned, direction):
        flat = returned.reshape(owners * chunk, lanes // owners, tile)
        inside = slot // chunk == index
        at = jnp.where(inside, owner_map * chunk + slot - index * chunk, 0)
        return jnp.where(inside[:, None, None], jnp.take(flat, at, axis=0), direction)

    direction = jnp.zeros((tiles, lanes // owners, tile), jnp.bfloat16)
    carried = ()
    for index, base in enumerate(range(0, slots, chunk)):
        grads = lax.all_gather(arrived[index], "dp", axis=0)
        if index:
            grads, returned = lax.optimization_barrier((grads, returned))
            direction = place(index - 1, returned, direction)
        result, *carried = step(
            base, chunk, info, grads, roots, left_roots[0], left_stats[0], right_stats[0], carried
        )
        returned = lax.all_to_all(result, "owner", split_axis=0, concat_axis=0, tiled=True)
    direction = place(slots // chunk - 1, returned, direction)
    new_left, new_right = carried
    return (direction, new_left[None], new_right[None])


def solution(mesh):
    placed = (
        P("dp", None, "owner", None),
        P(),
        P("owner", None, "dp", None),
        P("owner", None, "dp", None),
        P("owner", None, "dp", None),
        P("owner", None, "dp", None),
    )
    return jax.shard_map(
        inner,
        mesh=mesh,
        in_specs=placed,
        out_specs=(
            P(None, ("dp", "owner"), None),
            P("owner", None, "dp", None),
            P("owner", None, "dp", None),
        ),
        check_vma=False,
    )
```

time: 951 us -> 768 us (0.81)
  waiting for transfers between devices: 602 us -> 495 us
  local copies, waits for them, and re-layouts: 100 us -> 33.7 us
  matrix products: 65.6 us -> 0 us
  Pallas kernels: 0 us -> 60.9 us
  blocking collectives: 143 us -> 124 us
  starting transfers between devices: 5.05 us -> 22.1 us
    all_to_all x1 -> x5, waiting for transfers between devices: 98.1 us -> 28.9 us  [the longest x4 28.9 us: inner(): lax.all_to_all(result, 'owner', split_axis=0, concat_axis=0, tiled=True)]
    dot_general x3 -> x0, matrix products: 65.6 us -> none  [the longest x1 25 us: body(): jnp.einsum('srk,skc->src', left_part, lax.all_gather(right_roots[0], 'dp'...]
    pallas_call x0 -> x4, Pallas kernels: none -> 60.9 us  [step(): pl.pallas_call(functools.partial(step_kernel, base), grid_spec=pltpu.Pref...]
    reshape x3 -> x5, local copies, waits for them, and re-layouts: 44.2 us -> 0.41 us  [the longest x4 0.33 us: inner(): which.reshape(-1)]
    all_gather x1 -> x0, local copies, waits for them, and re-layouts: 34.1 us -> none  [body(): lax.all_gather(arrived, 'dp', axis=2, tiled=True).reshape(slots, tile, tile)]
    all_gather x2 -> x5, waiting for transfers between devices: 381 us -> 348 us  [the longest x1 194 us: inner(): roots = lax.all_gather(right_roots[0], 'dp', axis=0)]
    all_to_all x1 -> x3, blocking collectives: 143 us -> 124 us  [inner(): lax.all_to_all(jnp.where(mask, taken, jnp.zeros((), shares.dtype)), 'owne...]
    all_to_all x1 -> x5, starting transfers between devices: 4.93 us -> 21.9 us  [the longest x4 18.3 us: inner(): lax.all_to_all(result, 'owner', split_axis=0, concat_axis=0, tiled=True)]
  transfers between devices with their start and end apart: 4 -> 11, of which waited for: 4 -> 6; matrix products, arithmetic and copies ran while one was open for 12% -> 5% of each run, Pallas kernels for 0% -> 6%
where the time goes in v1:
time: 768 us; the launch traced here: 767 us
  waiting for transfers between devices  495 us (64%)
  blocking collectives  124 us (16%)
  Pallas kernels  60.9 us (8%)
  local copies, waits for them, and re-layouts  33.7 us (4%)
  starting transfers between devices  22.1 us (3%)
  other arithmetic  16.3 us (2%)
  between operations  14.4 us (2%)
    all_gather x1, waiting for transfers between devices, inner(): roots = lax.all_gather(right_roots[0], 'dp', axis=0)  194 us
    all_gather x4, waiting for transfers between devices, inner(): grads = lax.all_gather(arrived[index], 'dp', axis=0)  154 us
    all_to_all x3, blocking collectives, inner(): lax.all_to_all(jnp.where(mask, taken, jnp.zeros((), shares.dtype)), 'owne...  124 us
    reduce_scatter x1, waiting for transfers between devices, inner(): lax.psum_scatter(partial_grads[0], 'dp', scatter_dimension=2, tiled=True)  117 us
    pallas_call x4, Pallas kernels, step(): pl.pallas_call(functools.partial(step_kernel, base), grid_spec=pltpu.Pref...  60.9 us
    all_to_all x4, waiting for transfers between devices, inner(): lax.all_to_all(result, 'owner', split_axis=0, concat_axis=0, tiled=True)  28.9 us
    all_to_all x4, starting transfers between devices, inner(): lax.all_to_all(result, 'owner', split_axis=0, concat_axis=0, tiled=True)  18.3 us
  transfers between devices with their start and end apart: 11, of which 6 were waited for; matrix products, arithmetic and copies ran while one was open for 5% of the time, Pallas kernels for 6%

profile of v1, /device:TPU:0, one launch (start us, length us, event | category | flops | bytes accessed | tf_op | source)
XLA Modules:
  0.0 767.2 jit_solution(13832131457265380511)
XLA Ops:
  7.2 0.7 reduce-scatter.2.cloned.1.call-update
  8.0 0.2 convert_reduce_fusion
  8.2 0.3 fusion.3
  8.7 0.7 gather_fusion.3
  9.4 0.1 copy.52
  9.7 0.7 gather_fusion.6
  10.4 0.7 gather_fusion.5
  11.3 0.7 gather_fusion.8
  12.0 0.7 gather_fusion.9
  12.9 0.7 gather_fusion.11
  13.6 0.7 gather_fusion.12
  14.3 0.7 gather_fusion.2
  15.1 0.1 copy.56
  15.3 0.1 copy.59
  15.4 0.1 copy.63
  15.6 0.1 copy.66
  15.7 0.1 copy.70
  15.9 0.1 copy.73
  16.1 0.3 and_reduce_fusion
  17.4 0.1 broadcast_compare_fusion.7
  17.5 0.1 broadcast_compare_fusion.3
  17.6 116.8 %reduce-scatter.2.cloned.1.call-done = bf16[48,128,256]{2,1,0:T(8,128)(2,1)} async-done(((bf16[48,128,1024]{2,1,0:T(8,128)(2,1)}), bf16[48,128,256]{2,1,0:T(8,128)(2,1)}) %reduce-scatter.2.cloned.1.call-update) | async-done | bytes 3145744 | tf_op jit(solution)/shard_map/reduce_scatter | solution.py:135
  134.4 2.5 gather_fusion.13
  137.0 0.2 broadcast_select_fusion
  137.2 0.7 and_select_fusion
  137.9 42.3 %all_to_all.40 = bf16[8,3,128,256]{3,2,1,0:T(8,128)(2,1)} all-to-all(bf16[8,3,128,256]{3,2,1,0:T(8,128)(2,1)S(1)} %and_select_fusion), channel_id=1, replica_groups=mesh['dp'=4,'owner'=8] {'owner'}, dimensions={0} | all-to-all | bytes 3145728 | tf_op jit(solution)/shard_map/all_to_all | solution.py:153
  180.3 0.7 all-gather.10.cloned.1.call-update
  181.3 0.9 copy-done.1
  182.2 1.8 gather_fusion.10
  184.0 1.8 broadcast_select_fusion.1
  185.8 0.7 and_select_fusion.1
  186.6 40.9 %all_to_all.41 = bf16[8,3,128,256]{3,2,1,0:T(8,128)(2,1)} all-to-all(bf16[8,3,128,256]{3,2,1,0:T(8,128)(2,1)S(1)} %and_select_fusion.1), channel_id=1, replica_groups=mesh['dp'=4,'owner'=8] {'owner'}, dimensions={0} | all-to-all | bytes 3145728 | tf_op jit(solution)/shard_map/all_to_all | solution.py:153
  227.8 1.8 gather_fusion.7
  229.6 1.6 broadcast_select_fusion.2
  231.2 0.8 and_select_fusion.2
  232.0 40.9 %all_to_all.42 = bf16[8,3,128,256]{3,2,1,0:T(8,128)(2,1)} all-to-all(bf16[8,3,128,256]{3,2,1,0:T(8,128)(2,1)S(1)} %and_select_fusion.2), channel_id=1, replica_groups=mesh['dp'=4,'owner'=8] {'owner'}, dimensions={0} | all-to-all | bytes 3145728 | tf_op jit(solution)/shard_map/all_to_all | solution.py:153
  273.2 1.8 gather_fusion.4
  275.0 1.6 broadcast_select_fusion.3
  276.6 1.6 and_select_fusion.3
  278.2 3.6 all-to-all-start
  281.8 0.2 dynamic-slice_reduce_fusion
  282.0 0.7 gather_fusion
  282.7 0.7 gather_fusion.1
  283.4 0.1 copy.47
  283.7 194.2 %all-gather.10.cloned.1.call-done.roots = bf16[4,12,256,1024]{3,2,1,0:T(8,128)(2,1)} async-done(((bf16[1,12,256,1024]{3,2,1,0:T(8,128)(2,1)}), bf16[4,12,256,1024]{3,2,1,0:T(8,128)(2,1)}) %all-gather.10.cloned.1.call-update) | async-done | bytes 25165840 | tf_op jit(solution)/shard_map/all_gather | solution.py:136
  477.9 15.4 %shard_map.85 = (bf16[8,3,32,1024]{3,2,1,0:T(8,128)(2,1)}, f32[12,256,1024]{2,1,0:T(8,128)}, f32[12,256,1024]{2,1,0:T(8,128)}) custom-call(s32[25]{0:T(128)S(1)} %pad_add_fusion.1.info, bf16[4,8,3,128,256]{4,3,2,1,0:T(8,128)(2,1)} %bitcast.40, bf16[4,12,256,1024]{3,2,1,0:T(8,128)(2,1)} %all-gather.10.cloned.1.call-done.roots, ...), custom_call_target="tpu_custom_call" | custom-call | flops 6442450944 | bytes 28311552 | tf_op jit(solution)/shard_map/pallas_call | solution.py:86
  493.3 1.2 copy-done.2
  494.5 4.6 all-to-all-start.4
  499.1 0.5 all-gather.12.cloned.1.call-update
  499.6 50.1 %all-gather.16.cloned.1.call-done = bf16[32,3,128,256]{3,2,1,0:T(8,128)(2,1)} async-done(((bf16[8,3,128,256]{3,2,1,0:T(8,128)(2,1)}), bf16[32,3,128,256]{3,2,1,0:T(8,128)(2,1)}) %all-gather.16.cloned.1.call-update) | async-done | bytes 6291472 | tf_op jit(solution)/shard_map/all_gather | solution.py:171
  549.7 15.4 %shard_map.86 = (bf16[8,3,32,1024]{3,2,1,0:T(8,128)(2,1)}, f32[12,256,1024]{2,1,0:T(8,128)}, f32[12,256,1024]{2,1,0:T(8,128)}) custom-call(s32[25]{0:T(128)S(1)} %pad_add_fusion.1.info, bf16[4,8,3,128,256]{4,3,2,1,0:T(8,128)(2,1)} %bitcast.41, ...), custom_call_target="tpu_custom_call", output_to_operand_aliasing={{1}: (6, {}), {2}: (7, {})} | custom-call | flops 6442450944 | bytes 28311552 | tf_op jit(solution)/shard_map/pallas_call | solution.py:86
  565.1 4.6 all-to-all-start.5
  569.6 51.8 %all-gather.14.cloned.1.call-done = bf16[32,3,128,256]{3,2,1,0:T(8,128)(2,1)} async-done(((bf16[8,3,128,256]{3,2,1,0:T(8,128)(2,1)}), bf16[32,3,128,256]{3,2,1,0:T(8,128)(2,1)}) %all-gather.14.cloned.1.call-update) | async-done | bytes 6291472 | tf_op jit(solution)/shard_map/all_gather | solution.py:171
  621.4 15.4 %shard_map.87 = (bf16[8,3,32,1024]{3,2,1,0:T(8,128)(2,1)}, f32[12,256,1024]{2,1,0:T(8,128)}, f32[12,256,1024]{2,1,0:T(8,128)}) custom-call(s32[25]{0:T(128)S(1)} %pad_add_fusion.1.info, bf16[4,8,3,128,256]{4,3,2,1,0:T(8,128)(2,1)} %bitcast.42, ...), custom_call_target="tpu_custom_call", output_to_operand_aliasing={{1}: (6, {}), {2}: (7, {})} | custom-call | flops 6442450944 | bytes 28311552 | tf_op jit(solution)/shard_map/pallas_call | solution.py:86
  636.8 4.6 all-to-all-start.6
  641.4 51.8 %all-gather.12.cloned.1.call-done = bf16[32,3,128,256]{3,2,1,0:T(8,128)(2,1)} async-done(((bf16[8,3,128,256]{3,2,1,0:T(8,128)(2,1)}), bf16[32,3,128,256]{3,2,1,0:T(8,128)(2,1)}) %all-gather.12.cloned.1.call-update) | async-done | bytes 6291472 | tf_op jit(solution)/shard_map/all_gather | solution.py:171
  693.2 14.7 %shard_map.88 = (bf16[8,3,32,1024]{3,2,1,0:T(8,128)(2,1)}, f32[12,256,1024]{2,1,0:T(8,128)}, f32[12,256,1024]{2,1,0:T(8,128)}) custom-call(s32[25]{0:T(128)S(1)} %pad_add_fusion.1.info, bf16[4,8,3,128,256]{4,3,2,1,0:T(8,128)(2,1)} %bitcast.43, ...), custom_call_target="tpu_custom_call", output_to_operand_aliasing={{1}: (6, {}), {2}: (7, {})} | custom-call | flops 6442450944 | bytes 28311552 | tf_op jit(solution)/shard_map/pallas_call | solution.py:86
  707.9 4.6 all-to-all-start.7
  712.6 2.5 gather_fusion.17
  715.1 2.5 gather_fusion.16
  717.6 3.9 gather_fusion.15
  721.5 28.9 %all-to-all-done.7 = bf16[8,3,32,1024]{3,2,1,0:T(8,128)(2,1)} async-done(((bf16[8,3,32,1024]{3,2,1,0:T(8,128)(2,1)}), bf16[8,3,32,1024]{3,2,1,0:T(8,128)(2,1)}, u32[]{:S(2)}, u32[]{:S(2)}) %all-to-all-start.7) | async-done | bytes 1572896 | tf_op jit(solution)/shard_map/all_to_all | solution.py:178
  750.4 4.1 gather_fusion.14
  754.5 5.8 fusion.2
  (90 shorter events, 3.4 us)
Async XLA Ops:
  7.2 127.2 %reduce-scatter.2.cloned.1.call-start = ((), (), s32[]{:S(2)}) async-start(), calls=%async_computation.9 | async-start | bytes 15728640 | tf_op jit(solution)/shard_map/reduce_scatter | solution.py:135
  7.2 0.7 copy-start.3
  7.9 275.8 %all-gather.18.cloned.1.call-start = ((), (), s32[]{:S(2)}) async-start(), calls=%async_computation.14 | async-start | bytes 7864320 | tf_op jit(solution)/shard_map/all_gather | solution.py:171
  180.3 1.9 copy-start.1
  180.3 297.6 %all-gather.10.cloned.1.call-start = ((), (), s32[]{:S(2)}) async-start(), calls=%async_computation.10 | async-start | bytes 31457280 | tf_op jit(solution)/shard_map/all_gather | solution.py:136
  181.0 368.6 %all-gather.16.cloned.1.call-start = ((), (), s32[]{:S(2)}) async-start(), calls=%async_computation.13 | async-start | bytes 7864320 | tf_op jit(solution)/shard_map/all_gather | solution.py:171
  227.5 393.9 %all-gather.14.cloned.1.call-start = ((), (), s32[]{:S(2)}) async-start(), calls=%async_computation.12 | async-start | bytes 7864320 | tf_op jit(solution)/shard_map/all_gather | solution.py:171
  278.2 215.0 %all-to-all-start = ((bf16[8,3,128,256]{3,2,1,0:T(8,128)(2,1)}), bf16[8,3,128,256]{3,2,1,0:T(8,128)(2,1)S(1)}, u32[]{:S(2)}, u32[]{:S(2)}) async-start(bf16[8,3,128,256]{3,2,1,0:T(8,128)(2,1)} %and_select_fusion.3), calls=%async_computation.1 | async-start | bytes 3145728 | tf_op jit(solution)/shard_map/all_to_all | solution.py:153
  493.3 1.2 copy-start.2
  494.5 55.2 %all-to-all-start.4 = ((bf16[8,3,32,1024]{3,2,1,0:T(8,128)(2,1)}), bf16[8,3,32,1024]{3,2,1,0:T(8,128)(2,1)S(1)}, u32[]{:S(2)}, u32[]{:S(2)}) async-start(bf16[8,3,32,1024]{3,2,1,0:T(8,128)(2,1)} %get-tuple-element.25), calls=%async_computation.5 | async-start | bytes 3145728 | tf_op jit(solution)/shard_map/all_to_all | solution.py:178
  499.0 194.1 %all-gather.12.cloned.1.call-start = ((), (), s32[]{:S(2)}) async-start(), calls=%async_computation.11 | async-start | bytes 7864320 | tf_op jit(solution)/shard_map/all_gather | solution.py:171
  565.1 56.3 %all-to-all-start.5 = ((bf16[8,3,32,1024]{3,2,1,0:T(8,128)(2,1)}), bf16[8,3,32,1024]{3,2,1,0:T(8,128)(2,1)S(1)}, u32[]{:S(2)}, u32[]{:S(2)}) async-start(bf16[8,3,32,1024]{3,2,1,0:T(8,128)(2,1)} %get-tuple-element.29), calls=%async_computation.6 | async-start | bytes 3145728 | tf_op jit(solution)/shard_map/all_to_all | solution.py:178
  636.8 56.4 %all-to-all-start.6 = ((bf16[8,3,32,1024]{3,2,1,0:T(8,128)(2,1)}), bf16[8,3,32,1024]{3,2,1,0:T(8,128)(2,1)}, u32[]{:S(2)}, u32[]{:S(2)}) async-start(bf16[8,3,32,1024]{3,2,1,0:T(8,128)(2,1)} %get-tuple-element.33), calls=%async_computation.7 | async-start | bytes 3145728 | tf_op jit(solution)/shard_map/all_to_all | solution.py:178
  707.9 42.5 %all-to-all-start.7 = ((bf16[8,3,32,1024]{3,2,1,0:T(8,128)(2,1)}), bf16[8,3,32,1024]{3,2,1,0:T(8,128)(2,1)}, u32[]{:S(2)}, u32[]{:S(2)}) async-start(bf16[8,3,32,1024]{3,2,1,0:T(8,128)(2,1)} %get-tuple-element.37), calls=%async_computation.8 | async-start | bytes 3145728 | tf_op jit(solution)/shard_map/all_to_all | solution.py:178
  750.4 4.1 copy-start
Sparse Core Ops, SparseCore 0:
  11.1 123.2 reduce-scatter.1
  180.4 67.9 all-gather.17
  250.3 227.5 all-gather.9
  479.6 70.0 all-gather.15
  551.3 70.0 all-gather.13
  623.1 70.0 all-gather.11

commit v2 on v1

--- a/solution.py
+++ b/solution.py
@@ -12,8 +12,6 @@
 D_IN = 10576
 D_INNER = 5120
 TILE = 1024
-
-CHUNK = 3
 
 stat_decay = 0.999
 
@@ -111,6 +109,15 @@
     )(info, grads, roots, left_roots, left_stats, right_stats, *carried)
 
 
+def chunks_of(slots):
+    if slots < 6:
+        sizes = (slots,)
+    else:
+        last, middle = slots // 4, slots // 3
+        sizes = (slots - middle - last, middle, last)
+    return [(sum(sizes[:index]), size) for index, size in enumerate(sizes)]
+
+
 def inner(partial_grads, owner_map, left_stats, right_stats, left_roots, right_roots):
     dp = lax.axis_size("dp")
     owners = lax.axis_size("owner")
@@ -141,9 +148,9 @@
     info = jnp.stack([jnp.take(rows, tile_here) - dp_here * lanes, jnp.take(cols, tile_here)], 1)
     info = jnp.concatenate([dp_here[None], info.reshape(-1)]).astype(jnp.int32)
 
-    chunk = CHUNK if slots % CHUNK == 0 else 1
+    spans = chunks_of(slots)
     arrived = []
-    for base in range(0, slots, chunk):
+    for base, chunk in spans:
         which = tile_of[:, base : base + chunk]
         rows_of = jnp.where(filled[:, base : base + chunk], jnp.take(rows, which), 0)
         mask = (piece_rows[:, None] < rows_of[:, :, None, None]) & (
@@ -160,23 +167,24 @@
         arrived.append(sent)
 
     def place(index, returned, direction):
+        base, chunk = spans[index]
         flat = returned.reshape(owners * chunk, lanes // owners, tile)
-        inside = slot // chunk == index
-        at = jnp.where(inside, owner_map * chunk + slot - index * chunk, 0)
+        inside = (slot >= base) & (slot < base + chunk)
+        at = jnp.where(inside, owner_map * chunk + slot - base, 0)
         return jnp.where(inside[:, None, None], jnp.take(flat, at, axis=0), direction)
 
     direction = jnp.zeros((tiles, lanes // owners, tile), jnp.bfloat16)
     carried = ()
-    for index, base in enumerate(range(0, slots, chunk)):
+    for index, (base, chunk) in enumerate(spans):
         grads = lax.all_gather(arrived[index], "dp", axis=0)
         if index:
-            grads, returned = lax.optimization_barrier((grads, returned))
             direction = place(index - 1, returned, direction)
+            grads, direction = lax.optimization_barrier((grads, direction))
         result, *carried = step(
             base, chunk, info, grads, roots, left_roots[0], left_stats[0], right_stats[0], carried
         )
         returned = lax.all_to_all(result, "owner", split_axis=0, concat_axis=0, tiled=True)
-    direction = place(slots // chunk - 1, returned, direction)
+    direction = place(len(spans) - 1, returned, direction)
     new_left, new_right = carried
     return (direction, new_left[None], new_right[None])
 

time: 768 us -> 713 us (0.928)
  waiting for transfers between devices: 495 us -> 466 us
  local copies, waits for them, and re-layouts: 33.7 us -> 24.1 us
    all_to_all x4 -> x3, waiting for transfers between devices: 28.9 us -> 146 us  [inner(): lax.all_to_all(result, 'owner', split_axis=0, concat_axis=0, tiled=True)]
    all_gather x1, waiting for transfers between devices: 194 us -> 88.7 us  [inner(): roots = lax.all_gather(right_roots[0], 'dp', axis=0)]
    all_gather x4 -> x3, waiting for transfers between devices: 154 us -> 107 us  [inner(): grads = lax.all_gather(arrived[index], 'dp', axis=0)]
    select_n x1 -> x3, other arithmetic: 5.8 us -> 14.1 us  [place(): jnp.where(inside[:, None, None], jnp.take(flat, at, axis=0), direction)]
    all_to_all x3 -> x2, blocking collectives: 124 us -> 117 us  [inner(): lax.all_to_all(jnp.where(mask, taken, jnp.zeros((), shares.dtype)), 'owne...]
    pallas_call x4 -> x3, Pallas kernels: 60.9 us -> 54 us  [step(): pl.pallas_call(functools.partial(step_kernel, base), grid_spec=pltpu.Pref...]
    all_to_all x4 -> x3, starting transfers between devices: 18.3 us -> 11.5 us  [inner(): lax.all_to_all(result, 'owner', split_axis=0, concat_axis=0, tiled=True)]
  transfers between devices with their start and end apart: 11 -> 9, of which waited for: 6 -> 6; matrix products, arithmetic and copies ran while one was open for 5% -> 5% of each run, Pallas kernels for 6% -> 6%
where the time goes in v2:
time: 713 us; the launch traced here: 712 us
  waiting for transfers between devices  466 us (65%)
  blocking collectives  117 us (16%)
  Pallas kernels  54 us (8%)
  local copies, waits for them, and re-layouts  24.1 us (3%)
  other arithmetic  22.1 us (3%)
  starting transfers between devices  15.3 us (2%)
  between operations  14.1 us (2%)
    all_to_all x3, waiting for transfers between devices, inner(): lax.all_to_all(result, 'owner', split_axis=0, concat_axis=0, tiled=True)  146 us
    reduce_scatter x1, waiting for transfers between devices, inner(): lax.psum_scatter(partial_grads[0], 'dp', scatter_dimension=2, tiled=True)  122 us
    all_to_all x2, blocking collectives, inner(): lax.all_to_all(jnp.where(mask, taken, jnp.zeros((), shares.dtype)), 'owne...  117 us
    all_gather x3, waiting for transfers between devices, inner(): grads = lax.all_gather(arrived[index], 'dp', axis=0)  107 us
    all_gather x1, waiting for transfers between devices, inner(): roots = lax.all_gather(right_roots[0], 'dp', axis=0)  88.7 us
    pallas_call x3, Pallas kernels, step(): pl.pallas_call(functools.partial(step_kernel, base), grid_spec=pltpu.Pref...  54 us
  transfers between devices with their start and end apart: 9, of which 6 were waited for; matrix products, arithmetic and copies ran while one was open for 5% of the time, Pallas kernels for 6%

profile of v2, /device:TPU:0, one launch (start us, length us, event | category | flops | bytes accessed | tf_op | source)
XLA Modules:
  0.0 712.3 jit_solution(960396098691659030)
XLA Ops:
  7.2 0.7 reduce-scatter.2.cloned.1.call-update
  8.0 0.7 all-gather.8.cloned.1.call-update
  8.7 0.2 convert_reduce_fusion
  8.9 0.3 fusion
  9.2 0.1 copy.58
  9.4 0.8 gather_fusion.12
  10.3 0.1 copy.59
  10.4 0.8 gather_fusion.13
  11.2 0.1 copy.62
  11.3 0.3 and_reduce_fusion
  11.6 0.1 copy.64
  11.7 0.1 copy.63
  12.0 0.1 reshape.289
  12.3 122.1 %reduce-scatter.2.cloned.1.call-done = bf16[48,128,256]{2,1,0:T(8,128)(2,1)} async-done(((bf16[48,128,1024]{2,1,0:T(8,128)(2,1)}), bf16[48,128,256]{2,1,0:T(8,128)(2,1)}) %reduce-scatter.2.cloned.1.call-update) | async-done | bytes 3145744 | tf_op jit(solution)/shard_map/reduce_scatter | solution.py:142
  134.4 2.6 gather_fusion.2
  137.0 1.3 and_select_fusion
  138.3 64.8 %all_to_all.30 = bf16[8,5,128,256]{3,2,1,0:T(8,128)(2,1)} all-to-all(bf16[8,5,128,256]{3,2,1,0:T(8,128)(2,1)S(1)} %and_select_fusion), channel_id=1, replica_groups=mesh['dp'=4,'owner'=8] {'owner'}, dimensions={0} | all-to-all | bytes 5242880 | tf_op jit(solution)/shard_map/all_to_all | solution.py:160
  203.2 0.1 copy.50
  203.3 0.1 reshape.437
  203.4 0.7 gather_fusion.10
  204.1 0.7 gather_fusion.11
  204.9 0.1 copy.51
  205.0 0.1 copy.54
  205.2 0.1 copy.56
  205.3 0.1 copy.55
  205.5 0.1 reshape.288
  205.7 0.1 broadcast_compare_fusion.2
  205.8 0.2 copy-done
  206.0 2.0 gather_fusion.1
  208.0 2.3 and_select_fusion.1
  210.3 52.2 %all_to_all.31 = bf16[8,4,128,256]{3,2,1,0:T(8,128)(2,1)} all-to-all(bf16[8,4,128,256]{3,2,1,0:T(8,128)(2,1)S(1)} %and_select_fusion.1), channel_id=1, replica_groups=mesh['dp'=4,'owner'=8] {'owner'}, dimensions={0} | all-to-all | bytes 4194304 | tf_op jit(solution)/shard_map/all_to_all | solution.py:160
  262.7 0.7 gather_fusion.8
  263.4 0.7 gather_fusion.9
  264.2 0.1 copy.43
  264.4 0.1 copy.46
  264.5 0.1 copy.48
  264.6 0.1 copy.47
  265.1 1.8 gather_fusion
  266.9 2.8 and_select_fusion.2
  269.7 3.6 all-to-all-start
  273.3 0.2 dynamic-slice_reduce_fusion
  273.5 0.7 gather_fusion.6
  274.2 0.7 gather_fusion.7
  274.9 0.1 copy.41
  275.0 0.1 reshape.286
  275.1 88.7 %all-gather.8.cloned.1.call-done.roots = bf16[4,12,256,1024]{3,2,1,0:T(8,128)(2,1)} async-done(((bf16[1,12,256,1024]{3,2,1,0:T(8,128)(2,1)}), bf16[4,12,256,1024]{3,2,1,0:T(8,128)(2,1)}) %all-gather.8.cloned.1.call-update) | async-done | bytes 25165840 | tf_op jit(solution)/shard_map/all_gather | solution.py:143
  363.9 106.8 %all-gather.14.cloned.1.call-done = bf16[32,5,128,256]{3,2,1,0:T(8,128)(2,1)} async-done(((bf16[8,5,128,256]{3,2,1,0:T(8,128)(2,1)}), bf16[32,5,128,256]{3,2,1,0:T(8,128)(2,1)}) %all-gather.14.cloned.1.call-update) | async-done | bytes 10485776 | tf_op jit(solution)/shard_map/all_gather | solution.py:179
  470.7 22.2 %shard_map.85 = (bf16[8,5,32,1024]{3,2,1,0:T(8,128)(2,1)}, f32[12,256,1024]{2,1,0:T(8,128)}, f32[12,256,1024]{2,1,0:T(8,128)}) custom-call(s32[25]{0:T(128)S(1)} %pad_add_fusion.1.info, bf16[4,8,5,128,256]{4,3,2,1,0:T(8,128)(2,1)} %bitcast.41, bf16[4,12,256,1024]{3,2,1,0:T(8,128)(2,1)} %all-gather.8.cloned.1.call-done.roots, ...), custom_call_target="tpu_custom_call" | custom-call | flops 10737418240 | bytes 47185920 | tf_op jit(solution)/shard_map/pallas_call | solution.py:84
  492.9 1.1 copy-done.1
  494.1 4.1 all-to-all-start.3
  498.3 0.5 all-gather.10.cloned.1.call-update
  498.9 59.6 %all-to-all-done.3 = bf16[8,5,32,1024]{3,2,1,0:T(8,128)(2,1)S(1)} async-done(((bf16[8,5,32,1024]{3,2,1,0:T(8,128)(2,1)}), bf16[8,5,32,1024]{3,2,1,0:T(8,128)(2,1)S(1)}, u32[]{:S(2)}, u32[]{:S(2)}) %all-to-all-start.3) | async-done | bytes 2621472 | tf_op jit(solution)/shard_map/all_to_all | solution.py:186
  558.5 2.5 gather_fusion.3
  561.0 4.0 select_select_fusion.2
  565.0 17.1 %shard_map.86 = (bf16[8,4,32,1024]{3,2,1,0:T(8,128)(2,1)}, f32[12,256,1024]{2,1,0:T(8,128)}, f32[12,256,1024]{2,1,0:T(8,128)}) custom-call(s32[25]{0:T(128)S(1)} %pad_add_fusion.1.info, bf16[4,8,4,128,256]{4,3,2,1,0:T(8,128)(2,1)} %bitcast.43, ...), custom_call_target="tpu_custom_call", output_to_operand_aliasing={{1}: (6, {}), {2}: (7, {})} | custom-call | flops 8589934592 | bytes 37748736 | tf_op jit(solution)/shard_map/pallas_call | solution.py:84
  582.2 3.8 all-to-all-start.4
  586.0 48.8 %all-to-all-done.4 = bf16[8,4,32,1024]{3,2,1,0:T(8,128)(2,1)S(1)} async-done(((bf16[8,4,32,1024]{3,2,1,0:T(8,128)(2,1)}), bf16[8,4,32,1024]{3,2,1,0:T(8,128)(2,1)S(1)}, u32[]{:S(2)}, u32[]{:S(2)}) %all-to-all-start.4) | async-done | bytes 2097184 | tf_op jit(solution)/shard_map/all_to_all | solution.py:186
  634.7 2.5 gather_fusion.4
  637.2 5.0 select_select_fusion.1
  642.2 14.7 %shard_map.87 = (bf16[8,3,32,1024]{3,2,1,0:T(8,128)(2,1)}, f32[12,256,1024]{2,1,0:T(8,128)}, f32[12,256,1024]{2,1,0:T(8,128)}) custom-call(s32[25]{0:T(128)S(1)} %pad_add_fusion.1.info, bf16[4,8,3,128,256]{4,3,2,1,0:T(8,128)(2,1)} %bitcast.45, ...), custom_call_target="tpu_custom_call", output_to_operand_aliasing={{1}: (6, {}), {2}: (7, {})} | custom-call | flops 6442450944 | bytes 28311552 | tf_op jit(solution)/shard_map/pallas_call | solution.py:84
  656.9 3.6 all-to-all-start.5
  660.5 37.7 %all-to-all-done.5 = bf16[8,3,32,1024]{3,2,1,0:T(8,128)(2,1)S(1)} async-done(((bf16[8,3,32,1024]{3,2,1,0:T(8,128)(2,1)}), bf16[8,3,32,1024]{3,2,1,0:T(8,128)(2,1)S(1)}, u32[]{:S(2)}, u32[]{:S(2)}) %all-to-all-start.5) | async-done | bytes 1572896 | tf_op jit(solution)/shard_map/all_to_all | solution.py:186
  698.2 2.5 gather_fusion.5
  700.7 5.0 select_select_fusion
  (68 shorter events, 2.2 us)
Async XLA Ops:
  7.2 127.2 %reduce-scatter.2.cloned.1.call-start = ((), (), s32[]{:S(2)}) async-start(), calls=%async_computation.7 | async-start | bytes 15728640 | tf_op jit(solution)/shard_map/reduce_scatter | solution.py:142
  7.9 0.8 copy-start.2
  7.9 356.0 %all-gather.8.cloned.1.call-start = ((), (), s32[]{:S(2)}) async-start(), calls=%async_computation.8 | async-start | bytes 31457280 | tf_op jit(solution)/shard_map/all_gather | solution.py:143
  8.7 462.0 %all-gather.14.cloned.1.call-start = ((), (), s32[]{:S(2)}) async-start(), calls=%async_computation.11 | async-start | bytes 13107200 | tf_op jit(solution)/shard_map/all_gather | solution.py:179
  203.2 361.9 %all-gather.12.cloned.1.call-start = ((), (), s32[]{:S(2)}) async-start(), calls=%async_computation.10 | async-start | bytes 10485760 | tf_op jit(solution)/shard_map/all_gather | solution.py:179
  204.1 1.9 copy-start
  269.7 223.2 %all-to-all-start = ((bf16[8,3,128,256]{3,2,1,0:T(8,128)(2,1)}), bf16[8,3,128,256]{3,2,1,0:T(8,128)(2,1)S(1)}, u32[]{:S(2)}, u32[]{:S(2)}) async-start(bf16[8,3,128,256]{3,2,1,0:T(8,128)(2,1)} %and_select_fusion.2), calls=%async_computation.1 | async-start | bytes 3145728 | tf_op jit(solution)/shard_map/all_to_all | solution.py:160
  492.9 1.2 copy-start.1
  494.1 64.4 %all-to-all-start.3 = ((bf16[8,5,32,1024]{3,2,1,0:T(8,128)(2,1)}), bf16[8,5,32,1024]{3,2,1,0:T(8,128)(2,1)S(1)}, u32[]{:S(2)}, u32[]{:S(2)}) async-start(bf16[8,5,32,1024]{3,2,1,0:T(8,128)(2,1)} %get-tuple-element.20), calls=%async_computation.4 | async-start | bytes 5242880 | tf_op jit(solution)/shard_map/all_to_all | solution.py:186
  498.2 144.0 %all-gather.10.cloned.1.call-start = ((), (), s32[]{:S(2)}) async-start(), calls=%async_computation.9 | async-start | bytes 7864320 | tf_op jit(solution)/shard_map/all_gather | solution.py:179
  582.2 52.6 %all-to-all-start.4 = ((bf16[8,4,32,1024]{3,2,1,0:T(8,128)(2,1)}), bf16[8,4,32,1024]{3,2,1,0:T(8,128)(2,1)S(1)}, u32[]{:S(2)}, u32[]{:S(2)}) async-start(bf16[8,4,32,1024]{3,2,1,0:T(8,128)(2,1)} %get-tuple-element.24), calls=%async_computation.5 | async-start | bytes 4194304 | tf_op jit(solution)/shard_map/all_to_all | solution.py:186
  656.9 41.3 %all-to-all-start.5 = ((bf16[8,3,32,1024]{3,2,1,0:T(8,128)(2,1)}), bf16[8,3,32,1024]{3,2,1,0:T(8,128)(2,1)S(1)}, u32[]{:S(2)}, u32[]{:S(2)}) async-start(bf16[8,3,32,1024]{3,2,1,0:T(8,128)(2,1)} %get-tuple-element.29), calls=%async_computation.6 | async-start | bytes 3145728 | tf_op jit(solution)/shard_map/all_to_all | solution.py:186
Sparse Core Ops, SparseCore 0:
  11.1 123.2 reduce-scatter.1
  136.3 227.5 all-gather.7
  365.7 104.9 all-gather.13
  472.4 87.4 all-gather.11
  561.6 70.0 all-gather.9

commit v3 on v2

--- a/solution.py
+++ b/solution.py
@@ -40,8 +40,23 @@
     return lax.dot_general(a, b, (dims, ((), ())), preferred_element_type=jnp.float32)
 
 
-def step_kernel(base, info, grads, roots, left_roots, left_stats, right_stats, *rest):
-    direction, new_left, new_right, left_part = rest[-4:]
+def product_kernel(base, info, grads, roots, left_roots, direction, left_part):
+    dp, _, _, _, width = grads.shape
+    tile = roots.shape[-1]
+    for d in range(dp):
+        part = dot(left_roots[0], grads[d].reshape(tile, width), ((1,), (0,)))
+        left_part[:, d * width : (d + 1) * width] = part.astype(jnp.bfloat16)
+    product = dot(left_part[...], roots[...].reshape(tile, tile), ((1,), (0,)))
+    slot = base + pl.program_id(0)
+    row = lax.broadcasted_iota(jnp.int32, product.shape, 0)
+    col = lax.broadcasted_iota(jnp.int32, product.shape, 1)
+    keep = (row < info[1 + 2 * slot]) & (col < info[2 + 2 * slot])
+    result = jnp.where(keep, product, 0.0).astype(jnp.bfloat16)
+    direction[...] = result.reshape(direction.shape)
+
+
+def stats_kernel(info, grads, left_stats, right_stats, *rest):
+    new_left, new_right = rest[-2:]
     dp, _, _, piece, width = grads.shape
     lanes, tile = left_stats.shape[1:]
     here = info[0]
@@ -53,60 +68,72 @@
         right = dot(mine, full[d], ((1,), (0,)))
         cut = (0, slice(None), slice(d * width, (d + 1) * width))
         new_right[cut] = stat_decay * right_stats[cut] + (1.0 - stat_decay) * right
-        part = dot(left_roots[0], full[d], ((1,), (0,)))
-        left_part[:, d * width : (d + 1) * width] = part.astype(jnp.bfloat16)
         rows = grads[d, pl.ds(here * pieces, pieces)].reshape(lanes, width)
         term = dot(rows, full[d], ((1,), (1,)))
         gram = term if gram is None else gram + term
     new_left[0] = stat_decay * left_stats[0] + (1.0 - stat_decay) * gram
-    product = dot(left_part[...], roots[...].reshape(tile, tile), ((1,), (0,)))
-    slot = base + pl.program_id(0)
-    row = lax.broadcasted_iota(jnp.int32, product.shape, 0)
-    col = lax.broadcasted_iota(jnp.int32, product.shape, 1)
-    keep = (row < info[1 + 2 * slot]) & (col < info[2 + 2 * slot])
-    result = jnp.where(keep, product, 0.0).astype(jnp.bfloat16)
-    direction[...] = result.reshape(direction.shape)
-
-
-def step(base, chunk, info, grads, roots, left_roots, left_stats, right_stats, carried):
+
+
+def params():
+    return pltpu.CompilerParams(vmem_limit_bytes=48 * 1024 * 1024)
+
+
+def product_step(base, chunk, info, grads, roots, left_roots):
     dp, owners, _, piece, width = grads.shape
-    _, lanes, tile = left_stats.shape
-    at = lambda s, info: (base + s, 0, 0)
-    stats = pl.BlockSpec((1, lanes, tile), at)
-    in_specs = [
-        pl.BlockSpec((dp, owners, 1, piece, width), lambda s, info: (0, 0, s, 0, 0)),
-        pl.BlockSpec((dp, 1, lanes, tile), lambda s, info: (0, base + s, 0, 0)),
-        stats,
-        stats,
-        stats,
-    ] + [pl.BlockSpec(memory_space=pl.ANY)] * len(carried)
+    _, lanes, tile = left_roots.shape
     sub = lanes // owners
     return pl.pallas_call(
-        functools.partial(step_kernel, base),
+        functools.partial(product_kernel, base),
         grid_spec=pltpu.PrefetchScalarGridSpec(
             num_scalar_prefetch=1,
             grid=(chunk,),
-            in_specs=in_specs,
-            out_specs=[
-                pl.BlockSpec((owners, 1, sub, tile), lambda s, info: (0, s, 0, 0)),
+            in_specs=[
+                pl.BlockSpec((dp, owners, 1, piece, width), lambda s, info: (0, 0, s, 0, 0)),
+                pl.BlockSpec((dp, 1, lanes, tile), lambda s, info: (0, base + s, 0, 0)),
+                pl.BlockSpec((1, lanes, tile), lambda s, info: (base + s, 0, 0)),
+            ],
+            out_specs=pl.BlockSpec((owners, 1, sub, tile), lambda s, info: (0, s, 0, 0)),
+            scratch_shapes=[pltpu.VMEM((lanes, tile), jnp.bfloat16)],
+        ),
+        out_shape=jax.ShapeDtypeStruct((owners, chunk, sub, tile), jnp.bfloat16),
+        compiler_params=params(),
+        cost_estimate=pl.CostEstimate(
+            flops=4 * chunk * lanes * tile * tile,
+            bytes_accessed=chunk * (4 * tile * tile + 4 * lanes * tile),
+            transcendentals=0,
+        ),
+    )(info, grads, roots, left_roots)
+
+
+def stats_step(base, chunk, info, grads, left_stats, right_stats, carried):
+    dp, owners, _, piece, width = grads.shape
+    _, lanes, tile = left_stats.shape
+    stats = pl.BlockSpec((1, lanes, tile), lambda s, info: (base + s, 0, 0))
+    return pl.pallas_call(
+        stats_kernel,
+        grid_spec=pltpu.PrefetchScalarGridSpec(
+            num_scalar_prefetch=1,
+            grid=(chunk,),
+            in_specs=[
+                pl.BlockSpec((dp, owners, 1, piece, width), lambda s, info: (0, 0, s, 0, 0)),
                 stats,
                 stats,
-            ],
-            scratch_shapes=[pltpu.VMEM((lanes, tile), jnp.bfloat16)],
+            ]
+            + [pl.BlockSpec(memory_space=pl.ANY)] * len(carried),
+            out_specs=[stats, stats],
         ),
         out_shape=[
-            jax.ShapeDtypeStruct((owners, chunk, sub, tile), jnp.bfloat16),
             jax.ShapeDtypeStruct(left_stats.shape, jnp.float32),
             jax.ShapeDtypeStruct(right_stats.shape, jnp.float32),
         ],
-        input_output_aliases={6: 1, 7: 2} if carried else {},
-        compiler_params=pltpu.CompilerParams(vmem_limit_bytes=48 * 1024 * 1024),
+        input_output_aliases={4: 0, 5: 1} if carried else {},
+        compiler_params=params(),
         cost_estimate=pl.CostEstimate(
-            flops=8 * chunk * lanes * tile * tile,
-            bytes_accessed=chunk * (4 * tile * tile + 20 * lanes * tile),
+            flops=4 * chunk * lanes * tile * tile,
+            bytes_accessed=chunk * (2 * tile * tile + 16 * lanes * tile),
             transcendentals=0,
         ),
-    )(info, grads, roots, left_roots, left_stats, right_stats, *carried)
+    )(info, grads, left_stats, right_stats, *carried)
 
 
 def chunks_of(slots):
@@ -178,12 +205,13 @@
     for index, (base, chunk) in enumerate(spans):
         grads = lax.all_gather(arrived[index], "dp", axis=0)
         if index:
+            grads, returned = lax.optimization_barrier((grads, returned))
+        result = product_step(base, chunk, info, grads, roots, left_roots[0])
+        if index:
             direction = place(index - 1, returned, direction)
-            grads, direction = lax.optimization_barrier((grads, direction))
-        result, *carried = step(
-            base, chunk, info, grads, roots, left_roots[0], left_stats[0], right_stats[0], carried
-        )
         returned = lax.all_to_all(result, "owner", split_axis=0, concat_axis=0, tiled=True)
+        grads, direction, result = lax.optimization_barrier((grads, direction, result))
+        carried = stats_step(base, chunk, info, grads, left_stats[0], right_stats[0], carried)
     direction = place(len(spans) - 1, returned, direction)
     new_left, new_right = carried
     return (direction, new_left[None], new_right[None])

time: 713 us -> 715 us (level)
  waiting for transfers between devices: 466 us -> 446 us
  Pallas kernels: 54 us -> 69.8 us
    all_to_all x3, waiting for transfers between devices: 146 us -> 0.01 us  [inner(): lax.all_to_all(result, 'owner', split_axis=0, concat_axis=0, tiled=True)]
    all_gather x3, waiting for transfers between devices: 107 us -> 235 us  [inner(): grads = lax.all_gather(arrived[index], 'dp', axis=0)]
    all_gather x1, waiting for transfers between devices: 88.7 us -> 51.4 us  [inner(): roots = lax.all_gather(right_roots[0], 'dp', axis=0)]
    all_to_all x1, waiting for transfers between devices: 0.01 us -> 36.1 us  [inner(): lax.all_to_all(jnp.where(mask, taken, jnp.zeros((), shares.dtype)), 'owne...]
    pallas_call x3 -> x6, Pallas kernels: 54 us -> 69.8 us  [the longest x3 36.5 us: stats_step(): pl.pallas_call(stats_kernel, grid_spec=pltpu.PrefetchScalarGridSpec(num_s...]
  transfers between devices with their start and end apart: 9 -> 9, of which waited for: 6 -> 6; matrix products, arithmetic and copies ran while one was open for 5% -> 5% of each run, Pallas kernels for 6% -> 9%
where the time goes in v3:
time: 715 us; the launch traced here: 714 us
  waiting for transfers between devices  446 us (62%)
  blocking collectives  117 us (16%)
  Pallas kernels  69.8 us (10%)
  local copies, waits for them, and re-layouts  29.3 us (4%)
  other arithmetic  20.3 us (3%)
  starting transfers between devices  17.6 us (2%)
  between operations  14.1 us (2%)
    all_gather x3, waiting for transfers between devices, inner(): grads = lax.all_gather(arrived[index], 'dp', axis=0)  235 us
    reduce_scatter x1, waiting for transfers between devices, inner(): lax.psum_scatter(partial_grads[0], 'dp', scatter_dimension=2, tiled=True)  122 us
    all_to_all x2, blocking collectives, inner(): lax.all_to_all(jnp.where(mask, taken, jnp.zeros((), shares.dtype)), 'owne...  117 us
    all_gather x1, waiting for transfers between devices, inner(): roots = lax.all_gather(right_roots[0], 'dp', axis=0)  51.4 us
    pallas_call x3, Pallas kernels, stats_step(): pl.pallas_call(stats_kernel, grid_spec=pltpu.PrefetchScalarGridSpec(num_s...  36.5 us
    all_to_all x1, waiting for transfers between devices, inner(): lax.all_to_all(jnp.where(mask, taken, jnp.zeros((), shares.dtype)), 'owne...  36.1 us
    pallas_call x3, Pallas kernels, product_step(): pl.pallas_call(functools.partial(product_kernel, base), grid_spec=pltpu.P...  33.3 us
  transfers between devices with their start and end apart: 9, of which 6 were waited for; matrix products, arithmetic and copies ran while one was open for 5% of the time, Pallas kernels for 9%

profile of v3, /device:TPU:0, one launch (start us, length us, event | category | flops | bytes accessed | tf_op | source)
XLA Modules:
  0.0 714.0 jit_solution(10193178627868566785)
XLA Ops:
  7.2 0.7 reduce-scatter.2.cloned.1.call-update
  8.0 0.7 all-gather.8.cloned.1.call-update
  8.7 0.2 convert_reduce_fusion
  8.9 0.3 fusion
  9.2 0.1 copy.58
  9.4 0.8 gather_fusion.13
  10.2 0.8 gather_fusion.12
  11.1 0.1 copy.59
  11.2 0.3 and_reduce_fusion
  11.5 0.1 copy.60
  11.6 0.1 copy.64
  11.7 0.1 copy.62
  11.8 0.1 copy.63
  12.3 122.1 %reduce-scatter.2.cloned.1.call-done = bf16[48,128,256]{2,1,0:T(8,128)(2,1)} async-done(((bf16[48,128,1024]{2,1,0:T(8,128)(2,1)}), bf16[48,128,256]{2,1,0:T(8,128)(2,1)}) %reduce-scatter.2.cloned.1.call-update) | async-done | bytes 3145744 | tf_op jit(solution)/shard_map/reduce_scatter | solution.py:169
  134.4 2.6 gather_fusion.2
  137.0 1.3 and_select_fusion
  138.3 64.8 %all_to_all.30 = bf16[8,5,128,256]{3,2,1,0:T(8,128)(2,1)} all-to-all(bf16[8,5,128,256]{3,2,1,0:T(8,128)(2,1)S(1)} %and_select_fusion), channel_id=1, replica_groups=mesh['dp'=4,'owner'=8] {'owner'}, dimensions={0} | all-to-all | bytes 5242880 | tf_op jit(solution)/shard_map/all_to_all | solution.py:187
  203.4 0.7 gather_fusion.11
  204.1 0.7 gather_fusion.10
  204.9 0.1 copy.51
  205.0 0.1 copy.56
  205.2 0.1 copy.54
  205.3 0.1 copy.55
  205.8 0.2 copy-done.3
  206.0 2.0 gather_fusion.1
  208.0 2.3 and_select_fusion.1
  210.3 52.2 %all_to_all.31 = bf16[8,4,128,256]{3,2,1,0:T(8,128)(2,1)} all-to-all(bf16[8,4,128,256]{3,2,1,0:T(8,128)(2,1)S(1)} %and_select_fusion.1), channel_id=1, replica_groups=mesh['dp'=4,'owner'=8] {'owner'}, dimensions={0} | all-to-all | bytes 4194304 | tf_op jit(solution)/shard_map/all_to_all | solution.py:187
  262.7 0.7 gather_fusion.9
  263.4 0.7 gather_fusion.8
  264.2 0.1 copy.43
  264.3 0.1 copy.48
  264.5 0.1 copy.46
  264.6 0.1 copy.47
  265.1 1.8 gather_fusion
  266.9 2.8 and_select_fusion.2
  269.7 3.6 all-to-all-start
  273.3 0.2 dynamic-slice_reduce_fusion
  273.6 0.7 gather_fusion.7
  274.2 0.7 gather_fusion.6
  274.9 36.1 %all-to-all-done = bf16[8,3,128,256]{3,2,1,0:T(8,128)(2,1)S(1)} async-done(((bf16[8,3,128,256]{3,2,1,0:T(8,128)(2,1)}), bf16[8,3,128,256]{3,2,1,0:T(8,128)(2,1)S(1)}, u32[]{:S(2)}, u32[]{:S(2)}) %all-to-all-start) | async-done | bytes 1572896 | tf_op jit(solution)/shard_map/all_to_all | solution.py:187
  311.0 1.1 copy-done.4
  312.2 0.1 copy.41
  312.3 0.1 reshape.286
  312.5 51.4 %all-gather.8.cloned.1.call-done.roots = bf16[4,12,256,1024]{3,2,1,0:T(8,128)(2,1)} async-done(((bf16[1,12,256,1024]{3,2,1,0:T(8,128)(2,1)}), bf16[4,12,256,1024]{3,2,1,0:T(8,128)(2,1)}) %all-gather.8.cloned.1.call-update) | async-done | bytes 25165840 | tf_op jit(solution)/shard_map/all_gather | solution.py:170
  363.9 106.8 %all-gather.14.cloned.1.call-done = bf16[32,5,128,256]{3,2,1,0:T(8,128)(2,1)} async-done(((bf16[8,5,128,256]{3,2,1,0:T(8,128)(2,1)}), bf16[32,5,128,256]{3,2,1,0:T(8,128)(2,1)}) %all-gather.14.cloned.1.call-update) | async-done | bytes 10485776 | tf_op jit(solution)/shard_map/all_gather | solution.py:206
  470.7 13.6 %shard_map.85 = bf16[8,5,32,1024]{3,2,1,0:T(8,128)(2,1)} custom-call(s32[25]{0:T(128)S(1)} %pad_add_fusion.1.info, bf16[4,8,5,128,256]{4,3,2,1,0:T(8,128)(2,1)} %bitcast.37, bf16[4,12,256,1024]{3,2,1,0:T(8,128)(2,1)} %all-gather.8.cloned.1.call-done.roots, bf16[12,256,1024]{2,1,0:T(8,128)(2,1)} %bitcast.32), custom_call_target="tpu_custom_call" | custom-call | flops 5368709120 | bytes 26214400 | tf_op jit(solution)/shard_map/pallas_call | solution.py:85
  484.3 4.6 all-to-all-start.3
  488.9 71.0 %all-gather.12.cloned.1.call-done = bf16[32,4,128,256]{3,2,1,0:T(8,128)(2,1)} async-done(((bf16[8,4,128,256]{3,2,1,0:T(8,128)(2,1)}), bf16[32,4,128,256]{3,2,1,0:T(8,128)(2,1)}) %all-gather.12.cloned.1.call-update) | async-done | bytes 8388624 | tf_op jit(solution)/shard_map/all_gather | solution.py:206
  559.9 10.7 %shard_map.86 = bf16[8,4,32,1024]{3,2,1,0:T(8,128)(2,1)} custom-call(s32[25]{0:T(128)S(1)} %pad_add_fusion.1.info, bf16[4,8,4,128,256]{4,3,2,1,0:T(8,128)(2,1)} %bitcast.39, bf16[4,12,256,1024]{3,2,1,0:T(8,128)(2,1)} %all-gather.8.cloned.1.call-done.roots, bf16[12,256,1024]{2,1,0:T(8,128)(2,1)} %bitcast.33), custom_call_target="tpu_custom_call" | custom-call | flops 4294967296 | bytes 20971520 | tf_op jit(solution)/shard_map/pallas_call | solution.py:85
  570.6 4.6 all-to-all-start.4
  575.2 57.0 %all-gather.10.cloned.1.call-done = bf16[32,3,128,256]{3,2,1,0:T(8,128)(2,1)} async-done(((bf16[8,3,128,256]{3,2,1,0:T(8,128)(2,1)}), bf16[32,3,128,256]{3,2,1,0:T(8,128)(2,1)}) %all-gather.10.cloned.1.call-update) | async-done | bytes 6291472 | tf_op jit(solution)/shard_map/all_gather | solution.py:206
  632.3 9.0 %shard_map.87 = bf16[8,3,32,1024]{3,2,1,0:T(8,128)(2,1)} custom-call(s32[25]{0:T(128)S(1)} %pad_add_fusion.1.info, bf16[4,8,3,128,256]{4,3,2,1,0:T(8,128)(2,1)} %bitcast.41, bf16[4,12,256,1024]{3,2,1,0:T(8,128)(2,1)} %all-gather.8.cloned.1.call-done.roots, bf16[12,256,1024]{2,1,0:T(8,128)(2,1)} %bitcast.34), custom_call_target="tpu_custom_call" | custom-call | flops 3221225472 | bytes 15728640 | tf_op jit(solution)/shard_map/pallas_call | solution.py:85
  641.3 4.6 all-to-all-start.5
  645.9 14.9 %shard_map.88 = (f32[12,256,1024]{2,1,0:T(8,128)}, f32[12,256,1024]{2,1,0:T(8,128)}) custom-call(s32[25]{0:T(128)S(1)} %pad_add_fusion.1.info, bf16[4,8,5,128,256]{4,3,2,1,0:T(8,128)(2,1)} %bitcast.38, f32[12,256,1024]{2,1,0:T(8,128)} %bitcast.26, f32[12,256,1024]{2,1,0:T(8,128)} %bitcast.29), custom_call_target="tpu_custom_call" | custom-call | flops 5368709120 | bytes 31457280 | tf_op jit(solution)/shard_map/pallas_call | solution.py:112
  660.9 4.3 gather_fusion.5
  665.1 0.4 broadcast_in_dim.196
  665.5 1.5 copy-done.2
  667.0 2.2 select_select_fusion
  669.2 11.5 %shard_map.89 = (f32[12,256,1024]{2,1,0:T(8,128)}, f32[12,256,1024]{2,1,0:T(8,128)}) custom-call(s32[25]{0:T(128)S(1)} %pad_add_fusion.1.info, bf16[4,8,4,128,256]{4,3,2,1,0:T(8,128)(2,1)} %bitcast.40, f32[12,256,1024]{2,1,0:T(8,128)} %bitcast.27, f32[12,256,1024]{2,1,0:T(8,128)} %bitcast.30, ...), custom_call_target="tpu_custom_call", output_to_operand_aliasing={{0}: (4, {}), {1}: (5, {})} | custom-call | flops 4294967296 | bytes 25165824 | tf_op jit(solution)/shard_map/pallas_call | solution.py:112
  680.7 4.1 gather_fusion.4
  684.8 5.0 select_select_fusion.1
  689.8 10.1 %shard_map.90 = (f32[12,256,1024]{2,1,0:T(8,128)}, f32[12,256,1024]{2,1,0:T(8,128)}) custom-call(s32[25]{0:T(128)S(1)} %pad_add_fusion.1.info, bf16[4,8,3,128,256]{4,3,2,1,0:T(8,128)(2,1)} %bitcast.42, f32[12,256,1024]{2,1,0:T(8,128)} %bitcast.28, f32[12,256,1024]{2,1,0:T(8,128)} %bitcast.31, ...), custom_call_target="tpu_custom_call", output_to_operand_aliasing={{0}: (4, {}), {1}: (5, {})} | custom-call | flops 3221225472 | bytes 18874368 | tf_op jit(solution)/shard_map/pallas_call | solution.py:112
  699.9 2.5 gather_fusion.3
  702.4 5.0 select_select_fusion.2
  (77 shorter events, 2.6 us)
Async XLA Ops:
  7.2 127.2 %reduce-scatter.2.cloned.1.call-start = ((), (), s32[]{:S(2)}) async-start(), calls=%async_computation.7 | async-start | bytes 15728640 | tf_op jit(solution)/shard_map/reduce_scatter | solution.py:169
  7.9 0.8 copy-start.5
  7.9 356.0 %all-gather.8.cloned.1.call-start = ((), (), s32[]{:S(2)}) async-start(), calls=%async_computation.8 | async-start | bytes 31457280 | tf_op jit(solution)/shard_map/all_gather | solution.py:170
  8.7 462.0 %all-gather.14.cloned.1.call-start = ((), (), s32[]{:S(2)}) async-start(), calls=%async_computation.11 | async-start | bytes 13107200 | tf_op jit(solution)/shard_map/all_gather | solution.py:206
  203.2 356.8 %all-gather.12.cloned.1.call-start = ((), (), s32[]{:S(2)}) async-start(), calls=%async_computation.10 | async-start | bytes 10485760 | tf_op jit(solution)/shard_map/all_gather | solution.py:206
  204.1 1.9 copy-start.3
  269.7 41.3 %all-to-all-start = ((bf16[8,3,128,256]{3,2,1,0:T(8,128)(2,1)}), bf16[8,3,128,256]{3,2,1,0:T(8,128)(2,1)S(1)}, u32[]{:S(2)}, u32[]{:S(2)}) async-start(bf16[8,3,128,256]{3,2,1,0:T(8,128)(2,1)} %and_select_fusion.2), calls=%async_computation.1 | async-start | bytes 3145728 | tf_op jit(solution)/shard_map/all_to_all | solution.py:187
  273.3 359.0 %all-gather.10.cloned.1.call-start = ((), (), s32[]{:S(2)}) async-start(), calls=%async_computation.9 | async-start | bytes 7864320 | tf_op jit(solution)/shard_map/all_gather | solution.py:206
  311.0 1.1 copy-start.4
  484.3 75.6 %all-to-all-start.3 = ((bf16[8,5,32,1024]{3,2,1,0:T(8,128)(2,1)}), bf16[8,5,32,1024]{3,2,1,0:T(8,128)(2,1)S(1)}, u32[]{:S(2)}, u32[]{:S(2)}) async-start(bf16[8,5,32,1024]{3,2,1,0:T(8,128)(2,1)} %shard_map.85), calls=%async_computation.4 | async-start | bytes 5242880 | tf_op jit(solution)/shard_map/all_to_all | solution.py:212
  559.9 10.7 %copy-start.1 = (bf16[8,5,32,1024]{3,2,1,0:T(8,128)(2,1)}, bf16[8,5,32,1024]{3,2,1,0:T(8,128)(2,1)S(1)}, u32[]{:S(2)}) copy-start(bf16[8,5,32,1024]{3,2,1,0:T(8,128)(2,1)S(1)} %all-to-all-done.3) | copy-start | bytes 7864324
  570.6 61.6 %all-to-all-start.4 = ((bf16[8,4,32,1024]{3,2,1,0:T(8,128)(2,1)}), bf16[8,4,32,1024]{3,2,1,0:T(8,128)(2,1)S(1)}, u32[]{:S(2)}, u32[]{:S(2)}) async-start(bf16[8,4,32,1024]{3,2,1,0:T(8,128)(2,1)} %shard_map.86), calls=%async_computation.5 | async-start | bytes 4194304 | tf_op jit(solution)/shard_map/all_to_all | solution.py:212
  632.3 9.0 %copy-start = (bf16[8,4,32,1024]{3,2,1,0:T(8,128)(2,1)}, bf16[8,4,32,1024]{3,2,1,0:T(8,128)(2,1)S(1)}, u32[]{:S(2)}) copy-start(bf16[8,4,32,1024]{3,2,1,0:T(8,128)(2,1)S(1)} %all-to-all-done.4) | copy-start | bytes 6291460
  641.3 58.6 %all-to-all-start.5 = ((bf16[8,3,32,1024]{3,2,1,0:T(8,128)(2,1)}), bf16[8,3,32,1024]{3,2,1,0:T(8,128)(2,1)S(1)}, u32[]{:S(2)}, u32[]{:S(2)}) async-start(bf16[8,3,32,1024]{3,2,1,0:T(8,128)(2,1)} %shard_map.87), calls=%async_computation.6 | async-start | bytes 3145728 | tf_op jit(solution)/shard_map/all_to_all | solution.py:212
  665.1 1.9 copy-start.2
Sparse Core Ops, SparseCore 0:
  11.1 123.2 reduce-scatter.1
  136.3 227.5 all-gather.7
  365.7 104.9 all-gather.13
  472.4 87.4 all-gather.11
  562.2 70.0 all-gather.9
